TPU v7x, 32 devices: a whole 2x2x4 slice. The times are simulated.
32 devices in a mesh: row: 8 (over y, x, core), col: 4 (over z).
Axes of the slice: x: 2, y: 2, z: 4, core: 2. Of those that a mesh axis runs over, the one named last changes fastest.
Arguments:
- source: float32 [512, 512, 512], P('row', 'col'), may hold values from -8 to 8
- basis_x: float32 [512, 512], replicated, may hold values from -0.25 to 0.25
- basis_y: float32 [512, 512], replicated, may hold values from -0.25 to 0.25
- basis_z: float32 [512, 512], replicated, may hold values from -0.25 to 0.25
- eigen_x: float32 [512], replicated, may hold values from 0.1 to 10
- eigen_y: float32 [512], replicated, may hold values from 0.1 to 10
- eigen_z: float32 [512], replicated, may hold values from 0.1 to 10
Outputs:
- solution: float32 [512, 512, 512], P('row', 'col')
All inputs are finite; a program needn't handle non-finite values.
Results may differ from a plain program's by a relative error of at most 0.00007.
Values sent between devices are 32-bit elements; how exact they have to be, the bound alone decides.
A program may use at most 128 MiB of HBM per device.

v0:
```python
import jax
import jax.numpy as jnp
from jax import lax
from jax.experimental.layout import Layout, with_layout_constraint
from jax.sharding import PartitionSpec as P

FAST = lax.Precision.HIGH
FULL = lax.Precision.HIGHEST


def cuts(planes):
    if planes < 3:
        return [(p, 1) for p in range(planes)]
    first = max(1, planes * 2 // 16)
    last = max(1, planes * 6 // 16)
    return [(0, first), (first, planes - first - last), (planes - last, last)]


def local(source, basis_x, basis_y, basis_z, eigen_x, eigen_y, eigen_z):
    rows_n = lax.axis_size("row")
    cols_n = lax.axis_size("col")
    devices = rows_n * cols_n
    me = lax.axis_index("row") * cols_n + lax.axis_index("col")
    ax, by, nz = source.shape
    nx, ny = basis_x.shape[0], basis_y.shape[0]
    planes = nz // devices
    bz = basis_z.reshape(nz, devices, planes)
    ez = lax.dynamic_slice_in_dim(eigen_z, me * planes, planes, 0)
    exy = eigen_x[:, None] + eigen_y[None, :]
    pieces = cuts(planes)

    def columns(piece):
        start, count = piece
        return bz[:, :, start : start + count].reshape(nz, devices * count)

    def exchange(field):
        return lax.all_to_all(field, ("row", "col"), split_axis=0, concat_axis=0, tiled=True)

    def forward(piece):
        field = jnp.einsum("ck,abc->kab", columns(piece), source, precision=FAST)
        return with_layout_constraint(field, Layout(major_to_minor=(0, 1, 2)))

    def middle(piece, field):
        start, count = piece
        field = field.reshape(rows_n, cols_n, count, ax, by)
        field = field.transpose(2, 0, 3, 1, 4).reshape(count, nx, ny)
        field = jnp.einsum("xi,kxy->kiy", basis_x, field, precision=FULL)
        field = jnp.einsum("kiy,yj->kij", field, basis_y, precision=FULL)
        field = field / (exy[None] + ez[start : start + count][:, None, None])
        field = jnp.einsum("kij,yj->kiy", field, basis_y, precision=FULL)
        field = jnp.einsum("xi,kiy->kxy", basis_x, field, precision=FULL)
        field = field.reshape(count, rows_n, ax, cols_n, by).transpose(1, 3, 0, 2, 4)
        return field.reshape(devices * count, ax, by)

    def backward(piece, field, precision):
        return jnp.einsum("ck,kab->abc", columns(piece), field, precision=precision)

    count = len(pieces)
    tie = lax.optimization_barrier
    fields = [forward(pieces[0])]
    arrived = [exchange(fields[0])]
    done = []
    for n in range(1, count):
        field = forward(pieces[n])
        if done:
            arrived[-1], field, done[-1] = tie((arrived[-1], field, done[-1]))
        else:
            arrived[-1], field = tie((arrived[-1], field))
        arrived.append(exchange(field))
        done.append(middle(pieces[n - 1], arrived[n - 1]))
    if done:
        arrived[-1], *done = tie((arrived[-1], *done))
    returned = []
    for n, piece in enumerate(pieces):
        if n == count - 1:
            if count > 2:
                returned[0], arrived[-1] = tie((returned[0], arrived[-1]))
            done.append(middle(piece, arrived[-1]))
        field = done[n]
        if returned:
            returned[-1], field = tie((returned[-1], field))
        returned.append(exchange(field))
    total = backward(pieces[0], returned[0], FULL)
    for piece, field in zip(pieces[1:], returned[1:]):
        total = lax.optimization_barrier(total)
        last = piece is pieces[-1]
        total = total + backward(piece, field, FAST if last else FULL)
    return total


def solution(mesh):
    placed = (P("row", "col", None), P(), P(), P(), P(), P(), P())
    return jax.shard_map(
        local, mesh=mesh, in_specs=placed, out_specs=P("row", "col", None), check_vma=False
    )
```

profile of v0, /device:TPU:9, one launch (start us, length us, event | category | flops | bytes accessed | tf_op | source)
XLA Modules:
  0.0 818.5 jit_solution(13178592944855999106)
XLA Ops:
  0.0 0.0 copy-start
  0.0 1.6 copy.59
  1.7 0.0 copy-start.4
  1.7 0.1 reshape.97
  1.8 11.5 %fusion.41 = f32[64,64,128]{2,0,1:T(8,128)S(1)} fusion(f32[512,64,1]{0,1,2:T(8,128)S(1)} %reshape.97, f32[64,128,512]{2,1,0:T(8,128)} %param.7), kind=kOutput, calls=%fused_computation.51 | convolution fusion | flops 1610612736 | bytes 19005440 | tf_op jit(solution)/shard_map/ck,abc->kab/dot_general | solution.py:40
  13.4 2.5 copy.60
  15.9 7.0 all-to-all-start
  22.9 10.6 %fusion.40 = f32[256,64,128]{2,0,1:T(8,128)S(1)} fusion(f32[64,128,512]{2,1,0:T(8,128)} %param.7, f32[512,32,16]{0,2,1:T(8,128)} %bitcast.96), kind=kOutput, calls=%fused_computation.50 | convolution fusion | flops 6442450944 | bytes 25690112 | tf_op jit(solution)/shard_map/ck,abc->kab/dot_general | solution.py:40
  33.5 8.3 %copy.61 = f32[256,64,128]{2,1,0:T(8,128)} copy(f32[256,64,128]{2,0,1:T(8,128)S(1)} %fusion.40) | data formatting | bytes 16777216 | tf_op jit(solution)/shard_map/ck,abc->kab/dot_general | solution.py:40
  41.7 28.7 %all-to-all-done = f32[64,64,128]{2,1,0:T(8,128)S(1)} async-done(((f32[64,64,128]{2,1,0:T(8,128)}), f32[64,64,128]{2,1,0:T(8,128)S(1)}, u32[]{:S(2)}, u32[]{:S(2)}) %all-to-all-start) | async-done | bytes 2097184 | tf_op jit(solution)/shard_map/all_to_all | solution.py:37
  70.4 1.3 copy-done.3
  71.8 4.2 all-to-all-start.1
  76.0 1.1 slice.29
  77.1 0.1 reshape.99
  77.2 11.2 %fusion.42 = f32[192,64,128]{2,0,1:T(8,128)S(1)} fusion(f32[512,192,1]{0,1,2:T(8,128)S(1)} %reshape.99, f32[64,128,512]{2,1,0:T(8,128)} %param.7), kind=kOutput, calls=%fused_computation.52 | convolution fusion | flops 4831838208 | bytes 23461888 | tf_op jit(solution)/shard_map/ck,abc->kab/dot_general | solution.py:40
  88.3 0.0 copy-start.7
  88.3 0.0 copy-start.8
  88.4 6.3 copy.62
  94.6 0.8 dynamic_slice.3
  95.5 0.1 broadcast_add_fusion
  95.6 4.3 copy.107
  99.9 3.3 reshape.86
  103.2 0.0 copy-done.1
  103.2 5.0 fusion.36
  108.3 3.5 fusion.16
  111.8 3.8 fusion.20
  115.6 5.3 convolution_bitcast_fusion.2
  120.9 2.9 copy.67
  123.8 2.9 reshape.87
  126.7 3.3 copy.68
  130.0 131.9 %all-to-all-done.1 = f32[256,64,128]{2,1,0:T(8,128)} async-done(((f32[256,64,128]{2,1,0:T(8,128)}), f32[256,64,128]{2,1,0:T(8,128)}, u32[]{:S(2)}, u32[]{:S(2)}) %all-to-all-start.1) | async-done | bytes 8388640 | tf_op jit(solution)/shard_map/all_to_all | solution.py:37
  261.9 3.7 all-to-all-start.2
  265.6 0.1 slice.25
  265.7 14.8 %copy.105 = f32[8,4,8,64,128]{4,1,3,0,2:T(4,128)} copy(f32[8,4,8,64,128]{4,3,2,1,0:T(8,128)} %bitcast.11) | data formatting | bytes 16777216 | tf_op jit(solution)/shard_map/reshape | solution.py:45
  280.5 10.3 %reshape.90 = f32[8,512,512]{2,1,0:T(8,128)} reshape(f32[8,8,64,4,128]{4,3,2,1,0:T(4,128)} %bitcast.86) | data formatting | bytes 16777216 | tf_op jit(solution)/shard_map/reshape | solution.py:46
  290.8 15.7 %fusion.33 = f32[8,512,512]{2,1,0:T(8,128)S(1)} fusion(f32[8,512,512]{2,1,0:T(8,128)} %reshape.90, f32[512,512]{1,0:T(8,128)S(1)} %copy-done.1), kind=kOutput, calls=%fused_computation.41 | convolution fusion | flops 12884901888 | bytes 17825792 | tf_op jit(solution)/shard_map/xi,kxy->kiy/dot_general | solution.py:47
  306.4 13.6 %fusion = f32[8,512,512]{2,1,0:T(8,128)S(1)} fusion(f32[8,512,512]{2,1,0:T(8,128)S(1)} %fusion.33, f32[512,512]{1,0:T(8,128)S(1)} %copy-done), kind=kOutput, calls=%fused_computation.2 | convolution fusion | flops 12884901888 | bytes 17825792 | tf_op jit(solution)/shard_map/kiy,yj->kij/dot_general | solution.py:48
  320.0 15.2 %fusion.3 = f32[8,512,512]{1,2,0:T(8,128)S(1)} fusion(f32[8,512,512]{2,1,0:T(8,128)S(1)} %fusion, f32[8]{0:T(128)S(1)} %slice.25, f32[512,512]{1,0:T(8,128)S(1)} %broadcast_add_fusion, f32[512,512]{1,0:T(8,128)S(1)} %copy-done), kind=kOutput, calls=%fused_computation.6 | convolution fusion | flops 12889096192 | bytes 18874400 | tf_op jit(solution)/shard_map/kij,yj->kiy/dot_general | solution.py:50
  335.2 15.3 %convolution_bitcast_fusion = f32[8,512,512]{1,2,0:T(8,128)} fusion(f32[8,512,512]{1,2,0:T(8,128)S(1)} %fusion.3, f32[512,512]{1,0:T(8,128)S(1)} %copy-done.1), kind=kOutput, calls=%fused_computation.18 | convolution fusion | flops 12884901888 | bytes 17825792 | tf_op jit(solution)/shard_map/xi,kiy->kxy/dot_general | solution.py:51
  350.5 9.1 %copy.73 = f32[8,512,512]{2,1,0:T(8,128)} copy(f32[8,512,512]{1,2,0:T(8,128)} %convolution_bitcast_fusion) | data formatting | bytes 16777216 | tf_op jit(solution)/shard_map/xi,kiy->kxy/transpose | solution.py:51
  359.6 9.9 %reshape.91 = f32[8,8,64,4,128]{4,3,2,1,0:T(4,128)} reshape(f32[8,512,512]{2,1,0:T(8,128)} %copy.73) | data formatting | bytes 16777216 | tf_op jit(solution)/shard_map/reshape | solution.py:52
  369.5 7.9 copy.74
  377.4 28.3 %all-to-all-done.2 = f32[192,64,128]{2,1,0:T(8,128)} async-done(((f32[192,64,128]{2,1,0:T(8,128)}), f32[192,64,128]{2,1,0:T(8,128)}, u32[]{:S(2)}, u32[]{:S(2)}) %all-to-all-start.2) | async-done | bytes 6291488 | tf_op jit(solution)/shard_map/all_to_all | solution.py:37
  405.7 51.0 %all_to_all.30 = f32[64,64,128]{2,1,0:T(8,128)} all-to-all(f32[64,64,128]{2,1,0:T(8,128)} %bitcast.92), channel_id=1, replica_groups=mesh['row'=8,'col'=4] {'row','col'}, dimensions={0} | all-to-all | bytes 4194304 | tf_op jit(solution)/shard_map/all_to_all | solution.py:37
  456.7 5.2 all-to-all-start.4
  461.9 0.1 slice.26
  462.0 11.3 %copy.106 = f32[8,4,6,64,128]{4,1,3,0,2:T(4,128)} copy(f32[8,4,6,64,128]{4,3,2,1,0:T(8,128)} %bitcast.17) | data formatting | bytes 12582912 | tf_op jit(solution)/shard_map/reshape | solution.py:45
  473.2 7.8 reshape.94
  481.1 12.8 %fusion.30 = f32[6,512,512]{2,1,0:T(8,128)S(1)} fusion(f32[6,512,512]{2,1,0:T(8,128)} %reshape.94, f32[512,512]{1,0:T(8,128)S(1)} %copy-done.1), kind=kOutput, calls=%fused_computation.38 | convolution fusion | flops 9663676416 | bytes 13631488 | tf_op jit(solution)/shard_map/xi,kxy->kiy/dot_general | solution.py:47
  493.9 10.1 %fusion.6 = f32[6,512,512]{2,1,0:T(8,128)S(1)} fusion(f32[6,512,512]{2,1,0:T(8,128)S(1)} %fusion.30, f32[512,512]{1,0:T(8,128)S(1)} %copy-done), kind=kOutput, calls=%fused_computation.9 | convolution fusion | flops 9663676416 | bytes 13631488 | tf_op jit(solution)/shard_map/kiy,yj->kij/dot_general | solution.py:48
  504.0 11.5 %fusion.9 = f32[6,512,512]{1,2,0:T(8,128)S(1)} fusion(f32[6,512,512]{2,1,0:T(8,128)S(1)} %fusion.6, f32[6]{0:T(128)S(1)} %slice.26, f32[512,512]{1,0:T(8,128)S(1)} %broadcast_add_fusion, f32[512,512]{1,0:T(8,128)S(1)} %copy-done), kind=kOutput, calls=%fused_computation.13 | convolution fusion | flops 9666822144 | bytes 14680088 | tf_op jit(solution)/shard_map/kij,yj->kiy/dot_general | solution.py:50
  515.5 12.2 %convolution_bitcast_fusion.1 = f32[6,512,512]{1,2,0:T(8,128)} fusion(f32[6,512,512]{1,2,0:T(8,128)S(1)} %fusion.9, f32[512,512]{1,0:T(8,128)S(1)} %copy-done.1), kind=kOutput, calls=%fused_computation.21 | convolution fusion | flops 9663676416 | bytes 13631488 | tf_op jit(solution)/shard_map/xi,kiy->kxy/dot_general | solution.py:51
  527.8 6.5 copy.80
  534.3 7.5 reshape.95
  541.8 6.3 copy.81
  548.2 99.7 %all-to-all-done.4 = f32[256,64,128]{2,1,0:T(8,128)} async-done(((f32[256,64,128]{2,1,0:T(8,128)}), f32[256,64,128]{2,1,0:T(8,128)}, u32[]{:S(2)}, u32[]{:S(2)}) %all-to-all-start.4) | async-done | bytes 8388640 | tf_op jit(solution)/shard_map/all_to_all | solution.py:37
  647.8 3.7 all-to-all-start.5
  651.6 0.0 copy-done.2
  651.6 0.0 copy-start.5
  651.6 17.5 %fusion.18 = f32[64,128,512]{2,1,0:T(8,128)} fusion(f32[512,64,1]{0,1,2:T(8,128)} %copy-done.6, f32[64,64,128]{2,1,0:T(8,128)S(1)} %copy-done.2), kind=kOutput, calls=%fused_computation.24 | convolution fusion | flops 3221225472 | bytes 19005440 | tf_op jit(solution)/shard_map/ck,kab->abc/dot_general | solution.py:56
  669.1 0.0 copy-done.5
  669.1 28.9 %convolution_add_fusion.1 = f32[64,128,512]{2,1,0:T(8,128)} fusion(f32[64,128,512]{2,1,0:T(8,128)} %fusion.18, f32[256,64,128]{2,1,0:T(8,128)} %all-to-all-done.4, f32[512,32,16]{0,2,1:T(8,128)S(1)} %bitcast.98), kind=kOutput, calls=%fused_computation.1 | convolution fusion | flops 12889096192 | bytes 42467328 | tf_op jit(solution)/shard_map/ck,kab->abc/dot_general | solution.py:56
  698.0 93.6 %all-to-all-done.5 = f32[192,64,128]{2,1,0:T(8,128)} async-done(((f32[192,64,128]{2,1,0:T(8,128)}), f32[192,64,128]{2,1,0:T(8,128)}, u32[]{:S(2)}, u32[]{:S(2)}) %all-to-all-start.5) | async-done | bytes 6291488 | tf_op jit(solution)/shard_map/all_to_all | solution.py:37
  791.6 26.6 %convolution_add_fusion = f32[64,128,512]{2,1,0:T(8,128)} fusion(f32[64,128,512]{2,1,0:T(8,128)} %convolution_add_fusion.1, f32[512,192,1]{0,1,2:T(8,128)S(1)} %reshape.99, f32[192,64,128]{2,1,0:T(8,128)} %all-to-all-done.5), kind=kOutput, calls=%fused_computation | convolution fusion | flops 4836032512 | bytes 40239104 | tf_op jit(solution)/shard_map/ck,kab->abc/dot_general | solution.py:56
  (10 shorter events, 0.1 us)
Async XLA Ops:
  0.0 108.3 %copy-start = (f32[512,512]{1,0:T(8,128)S(1)}, f32[512,512]{1,0:T(8,128)}, u32[]{:S(2)}) copy-start(f32[512,512]{1,0:T(8,128)} %param.9) | copy-start | bytes 3145732
  1.7 11.7 %copy-start.4 = (f32[512,512]{0,1:T(8,128)}, f32[512,512]{0,1:T(8,128)S(1)}, u32[]{:S(2)}) copy-start(f32[512,512]{0,1:T(8,128)S(1)} %copy.59) | copy-start | bytes 3145732
  1.8 11.6 %copy-start.6 = (f32[512,64,1]{0,1,2:T(8,128)}, f32[512,64,1]{0,1,2:T(8,128)S(1)}, u32[]{:S(2)}) copy-start(f32[512,64,1]{0,1,2:T(8,128)S(1)} %reshape.97) | copy-start | bytes 393220
  15.9 54.5 %all-to-all-start = ((f32[64,64,128]{2,1,0:T(8,128)}), f32[64,64,128]{2,1,0:T(8,128)S(1)}, u32[]{:S(2)}, u32[]{:S(2)}) async-start(f32[64,64,128]{2,1,0:T(8,128)} %copy.60), calls=%async_computation | async-start | bytes 4194304 | tf_op jit(solution)/shard_map/all_to_all | solution.py:37
  70.4 1.3 copy-start.3
  71.8 190.1 %all-to-all-start.1 = ((f32[256,64,128]{2,1,0:T(8,128)}), f32[256,64,128]{2,1,0:T(8,128)}, u32[]{:S(2)}, u32[]{:S(2)}) async-start(f32[256,64,128]{2,1,0:T(8,128)} %copy.61), calls=%async_computation.1 | async-start | bytes 16777216 | tf_op jit(solution)/shard_map/all_to_all | solution.py:37
  88.3 7.1 copy-start.7
  88.3 7.1 copy-start.8
  94.6 8.6 %copy-start.1 = (f32[512,512]{1,0:T(8,128)S(1)}, f32[512,512]{1,0:T(8,128)}, u32[]{:S(2)}) copy-start(f32[512,512]{1,0:T(8,128)} %param.8) | copy-start | bytes 3145732
  261.9 143.8 %all-to-all-start.2 = ((f32[192,64,128]{2,1,0:T(8,128)}), f32[192,64,128]{2,1,0:T(8,128)}, u32[]{:S(2)}, u32[]{:S(2)}) async-start(f32[192,64,128]{2,1,0:T(8,128)} %copy.62), calls=%async_computation.2 | async-start | bytes 12582912 | tf_op jit(solution)/shard_map/all_to_all | solution.py:37
  456.7 191.2 %all-to-all-start.4 = ((f32[256,64,128]{2,1,0:T(8,128)}), f32[256,64,128]{2,1,0:T(8,128)}, u32[]{:S(2)}, u32[]{:S(2)}) async-start(f32[256,64,128]{2,1,0:T(8,128)} %bitcast.85), calls=%async_computation.4 | async-start | bytes 16777216 | tf_op jit(solution)/shard_map/all_to_all | solution.py:37
  647.8 3.7 copy-start.2
  647.8 143.8 %all-to-all-start.5 = ((f32[192,64,128]{2,1,0:T(8,128)}), f32[192,64,128]{2,1,0:T(8,128)}, u32[]{:S(2)}, u32[]{:S(2)}) async-start(f32[192,64,128]{2,1,0:T(8,128)} %bitcast.88), calls=%async_computation.5 | async-start | bytes 12582912 | tf_op jit(solution)/shard_map/all_to_all | solution.py:37
  651.6 17.5 %copy-start.5 = (f32[512,512]{0,1:T(8,128)S(1)}, f32[512,512]{0,1:T(8,128)}, u32[]{:S(2)}) copy-start(f32[512,512]{0,1:T(8,128)} %copy-done.4) | copy-start | bytes 3145732
where the time goes:
time: 824 us; the launch traced here: 818 us
  waiting for transfers between devices  382 us (46%)
  matrix products  230 us (28%)
  local copies, waits for them, and re-layouts  131 us (16%)
  blocking collectives  51 us (6%)
  starting transfers between devices  23.8 us (3%)
    all_to_all x5, waiting for transfers between devices, exchange(): lax.all_to_all(field, ('row', 'col'), split_axis=0, concat_axis=0, tiled=...  382 us
    dot_general x3, matrix products, backward(): return jnp.einsum('ck,kab->abc', columns(piece), field, precision=precision)  73 us
    all_to_all x1, blocking collectives, exchange(): lax.all_to_all(field, ('row', 'col'), split_axis=0, concat_axis=0, tiled=...  51 us
    dot_general x3, matrix products, middle(): field = jnp.einsum('xi,kxy->kiy', basis_x, field, precision=FULL)  33.5 us
    dot_general x3, matrix products, forward(): field = jnp.einsum('ck,abc->kab', columns(piece), source, precision=FAST)  33.3 us
    dot_general x3, matrix products, middle(): field = jnp.einsum('xi,kiy->kxy', basis_x, field, precision=FULL)  32.8 us
    dot_general x3, matrix products, middle(): field = jnp.einsum('kij,yj->kiy', field, basis_y, precision=FULL)  30.5 us
    reshape x3, local copies, waits for them, and re-layouts, middle(): field = field.reshape(rows_n, cols_n, count, ax, by)  30.3 us
  transfers between devices with their start and end apart: 5, of which 5 were waited for; matrix products, arithmetic and copies ran while one was open for 39% of the time, Pallas kernels for 0%

commit v1 on v0

--- a/solution.py
+++ b/solution.py
@@ -1,11 +1,235 @@
+import functools
+
 import jax
 import jax.numpy as jnp
 from jax import lax
+from jax.experimental import pallas as pl
 from jax.experimental.layout import Layout, with_layout_constraint
+from jax.experimental.pallas import tpu as pltpu
 from jax.sharding import PartitionSpec as P
 
 FAST = lax.Precision.HIGH
 FULL = lax.Precision.HIGHEST
+MESH = pl.DeviceIdType.MESH
+LANES = 128
+SUB = 8
+LIMIT = 46 << 20
+OUT_SHAPE = pltpu.VMEM
+
+
+def split(value):
+    high = value.astype(jnp.bfloat16)
+    low = (value - high.astype(jnp.float32)).astype(jnp.bfloat16)
+    return high, low
+
+
+def product(left, right, dims=((1,), (0,))):
+    dot = functools.partial(
+        lax.dot_general, dimension_numbers=(dims, ((), ())), preferred_element_type=jnp.float32
+    )
+    (lh, ll), (rh, rl) = left, right
+    return dot(lh, rh) + (dot(lh, rl) + dot(ll, rh))
+
+
+def partners(rows_n, cols_n):
+    half = cols_n // 2
+    near, far = list(range(half)), list(range(half, cols_n))
+    return [(r, c) for r in range(rows_n) for c in far] + [
+        (r, c) for r in range(rows_n) for c in reversed(near)
+    ]
+
+
+def fused(
+    rows_n, cols_n,
+    source, basis_x, basis_y, basis_z, eigen_x, eigen_y, eigen_z,
+    out,
+    stage, arrived, z_high, z_low, x_high, x_low, xt_high, xt_low, y_high, y_low, yt_high, yt_low,
+    exy, load_sem, basis_sem, send1, recv1, send2, recv2, credit,
+):
+    ax, by, nz = source.shape
+    devices = rows_n * cols_n
+    planes, _, nx, _ = stage.shape
+    chunks, groups = planes // SUB, ax // SUB
+    part = devices * SUB
+    row, col = lax.axis_index("row"), lax.axis_index("col")
+    me = row * cols_n + col
+    order = partners(rows_n, cols_n)
+    stage_flat = stage.reshape(planes * cols_n * nx, by)
+    arrived_flat = arrived.reshape(planes * cols_n * nx, by)
+    lines = arrived.reshape(chunks, devices, SUB, ax, by)
+    chunk_rows = SUB * cols_n * nx
+
+    def load(step, slot):
+        g = lax.rem(step, groups)
+        return pltpu.make_async_copy(
+            source.at[pl.ds(g * SUB, SUB)], out.at[pl.ds(slot * SUB, SUB)], load_sem.at[slot]
+        )
+
+    side = nx // by
+
+    def basis_at(n):
+        return pl.ds(2 * SUB + n * side, side)
+
+    def basis_copy(ref, n):
+        return pltpu.make_async_copy(ref.reshape(side, by, ref.shape[1]), out.at[basis_at(n)], basis_sem.at[n])
+
+    basis_copy(basis_z, 0).start()
+    load(0, 0).start()
+    load(1, 1).start()
+    basis_copy(basis_x, 1).start()
+    basis_copy(basis_y, 2).start()
+
+    barrier = pltpu.get_barrier_semaphore()
+    for r, c in order:
+        if r or c:
+            pl.semaphore_signal(barrier, inc=1, device_id=(row ^ r, col ^ c), device_id_type=MESH)
+
+    basis_copy(basis_z, 0).wait()
+    turned = out[basis_at(0)].reshape(nz, nz).T
+    for h in range(chunks):
+        rows = [turned[d * planes + h * SUB :][:SUB] for d in range(devices)]
+        z_high[h], z_low[h] = split(jnp.concatenate(rows, axis=0))
+
+    def exchange(make_src, make_dst, send_sem, recv_sem):
+        for r, c in order:
+            r2, c2 = row ^ r, col ^ c
+            if r or c:
+                pltpu.make_async_remote_copy(
+                    src_ref=make_src(r2, c2), dst_ref=make_dst(), send_sem=send_sem,
+                    recv_sem=recv_sem, device_id=(r2, c2), device_id_type=MESH,
+                ).start()
+            else:
+                pltpu.make_async_copy(make_src(r2, c2), make_dst(), recv_sem).start()
+
+    def block(ref, h, r, c, g):
+        start = pl.multiple_of(r * ax + g * SUB, SUB)
+        return ref.at[pl.ds(h * SUB, SUB), c, pl.ds(start, SUB), :]
+
+    def wait_rows(ref, count, sem):
+        view = ref.at[pl.ds(0, count)]
+        pltpu.make_async_copy(view, view, sem).wait()
+
+    pl.semaphore_wait(barrier, devices - 1)
+
+    @pl.loop(0, chunks * groups)
+    def _(step):
+        h, g, slot = step // groups, lax.rem(step, groups), lax.rem(step, 2)
+        load(step, slot).wait()
+
+        @pl.loop(0, SUB // 2)
+        def _(pair):
+            a = pair * 2
+            lhs = (z_high[h], z_low[h])
+            rhs = split(out[pl.ds(slot * SUB + a, 2)].reshape(2 * by, nz))
+            field = product(lhs, rhs, ((1,), (1,)))
+            for n in range(2):
+                for d in range(devices):
+                    start = h * chunk_rows + (d % cols_n) * nx + (d // cols_n) * ax + g * SUB + a + n
+                    stage_flat[pl.ds(start, SUB, stride=cols_n * nx), :] = field[
+                        d * SUB : (d + 1) * SUB, n * by : (n + 1) * by
+                    ]
+
+        @pl.when(step + 2 < chunks * groups)
+        def _():
+            load(step + 2, slot).start()
+
+        exchange(
+            lambda r, c: block(stage, h, r, c, g),
+            lambda: block(arrived, h, row, col, g),
+            send1.at[h], recv1.at[h],
+        )
+
+    basis_copy(basis_x, 1).wait()
+    basis_copy(basis_y, 2).wait()
+    for n, natural, turned_refs in ((1, (x_high, x_low), (xt_high, xt_low)), (2, (y_high, y_low), (yt_high, yt_low))):
+        value = out[basis_at(n)].reshape(nx, nx)
+        natural[0][...], natural[1][...] = split(value)
+        turned_refs[0][...], turned_refs[1][...] = split(value.T)
+    exy[...] = jnp.broadcast_to(eigen_x[...], exy.shape).T + eigen_y[...]
+
+    def both(pair):
+        return pair[0][...], pair[1][...]
+
+    for h in range(chunks):
+        wait_rows(arrived_flat, chunk_rows, recv1.at[h])
+        wait_rows(stage_flat, (devices - 1) * SUB * ax, send1.at[h])
+
+        @pl.loop(h * SUB, (h + 1) * SUB)
+        def _(p):
+            field = jnp.concatenate([arrived[p, c] for c in range(cols_n)], axis=1)
+            field = product(both((xt_high, xt_low)), split(field))
+            field = product(split(field), both((y_high, y_low)))
+            field = field / (exy[...] + eigen_z[me * planes + p])
+            field = product(split(field), both((yt_high, yt_low)))
+            field = product(both((x_high, x_low)), split(field))
+            for c in range(cols_n):
+                stage[p, c] = field[:, c * by : (c + 1) * by]
+
+        for r, c in order:
+            if r or c:
+                pl.semaphore_signal(credit.at[h], inc=1, device_id=(row ^ r, col ^ c), device_id_type=MESH)
+        pl.semaphore_wait(credit.at[h], devices - 1)
+
+        @pl.loop(0, groups)
+        def _(g):
+            exchange(
+                lambda r, c: block(stage, h, r, c, g),
+                lambda: lines.at[h, me, :, pl.ds(g * SUB, SUB), :],
+                send2.at[h], recv2.at[h, g],
+            )
+
+    for h in range(chunks):
+
+        @pl.loop(0, groups)
+        def _(g):
+            wait_rows(arrived_flat, part * SUB, recv2.at[h, g])
+
+            @pl.loop(0, SUB // 2)
+            def _(pair):
+                a = g * SUB + pair * 2
+                sides = [
+                    arrived_flat[pl.ds(h * chunk_rows + a + n, part, stride=ax), :].T for n in range(2)
+                ]
+                lhs = split(jnp.concatenate(sides, axis=0))
+                field = product(lhs, (z_high[h], z_low[h])).reshape(2, by, nz)
+                if h:
+                    out[pl.ds(a, 2)] += field
+                else:
+                    out[pl.ds(a, 2)] = field
+
+    for h in range(chunks):
+        wait_rows(stage_flat, (devices - 1) * SUB * ax, send2.at[h])
+
+
+def fused_local(source, basis_x, basis_y, basis_z, eigen_x, eigen_y, eigen_z):
+    rows_n, cols_n = lax.axis_size("row"), lax.axis_size("col")
+    devices = rows_n * cols_n
+    ax, by, nz = source.shape
+    nx, ny = basis_x.shape[0], basis_y.shape[0]
+    planes = nz // devices
+    chunks, groups = planes // SUB, ax // SUB
+    dma, any_space = pltpu.SemaphoreType.DMA, pl.BlockSpec(memory_space=pl.ANY)
+    vmem, smem = pl.BlockSpec(memory_space=pltpu.VMEM), pl.BlockSpec(memory_space=pltpu.SMEM)
+    field = pltpu.VMEM((planes, cols_n, nx, by), jnp.float32)
+    zb = pltpu.VMEM((chunks, devices * SUB, nz), jnp.bfloat16)
+    xb = pltpu.VMEM((nx, nx), jnp.bfloat16)
+    yb = pltpu.VMEM((ny, ny), jnp.bfloat16)
+    result = pl.pallas_call(
+        functools.partial(fused, rows_n, cols_n),
+        out_shape=OUT_SHAPE((ax, by, nz), jnp.float32),
+        in_specs=[any_space] * 4 + [vmem, vmem, smem],
+        out_specs=vmem,
+        scratch_shapes=[
+            field, field, zb, zb, xb, xb, xb, xb, yb, yb, yb, yb,
+            pltpu.VMEM((nx, ny), jnp.float32),
+            dma((2,)), dma((3,)), dma((chunks,)), dma((chunks,)), dma((chunks,)), dma((chunks, groups)),
+            pltpu.SemaphoreType.REGULAR((chunks,)),
+        ],
+        compiler_params=pltpu.CompilerParams(
+            collective_id=0, has_side_effects=True, vmem_limit_bytes=LIMIT
+        ),
+    )(source, basis_x, basis_y, basis_z, eigen_x[None], eigen_y[None], eigen_z)
+    return result
 
 
 def cuts(planes):
@@ -16,7 +240,7 @@
     return [(0, first), (first, planes - first - last), (planes - last, last)]
 
 
-def local(source, basis_x, basis_y, basis_z, eigen_x, eigen_y, eigen_z):
+def staged_local(source, basis_x, basis_y, basis_z, eigen_x, eigen_y, eigen_z):
     rows_n = lax.axis_size("row")
     cols_n = lax.axis_size("col")
     devices = rows_n * cols_n
@@ -89,6 +313,17 @@
 
 
 def solution(mesh):
+    rows_n, cols_n = mesh.shape["row"], mesh.shape["col"]
+
+    def local(source, basis_x, basis_y, basis_z, *eigen):
+        ax, by, nz = source.shape
+        square = basis_x.shape == basis_y.shape == basis_z.shape
+        planes = nz // (rows_n * cols_n)
+        power = not (rows_n & (rows_n - 1) or cols_n & (cols_n - 1))
+        fits = by == LANES and ax % SUB == 0 and planes % SUB == 0
+        body = fused_local if square and power and fits else staged_local
+        return body(source, basis_x, basis_y, basis_z, *eigen)
+
     placed = (P("row", "col", None), P(), P(), P(), P(), P(), P())
     return jax.shard_map(
         local, mesh=mesh, in_specs=placed, out_specs=P("row", "col", None), check_vma=False

time: 824 us -> 739 us (0.90)
  Pallas kernels: 0 us -> 731 us
  waiting for transfers between devices: 382 us -> 0 us
  matrix products: 230 us -> 0 us
  local copies, waits for them, and re-layouts: 131 us -> 6.16 us
  blocking collectives: 51 us -> 0 us
  starting transfers between devices: 23.8 us -> 0 us
    pallas_call x0 -> x1, Pallas kernels: none -> 731 us  [fused_local(): pl.pallas_call(functools.partial(fused, rows_n, cols_n), out_shape=OUT_SH...]
    all_to_all x5 -> x0, waiting for transfers between devices: 382 us -> none  [exchange(): lax.all_to_all(field, ('row', 'col'), split_axis=0, concat_axis=0, tiled=...]
    dot_general x18 -> x0, matrix products: 230 us -> none  [the longest x3 73 us: backward(): return jnp.einsum('ck,kab->abc', columns(piece), field, precision=precision)]
    reshape x11 -> x0, local copies, waits for them, and re-layouts: 72.2 us -> none  [the longest x3 30.3 us: middle(): field = field.reshape(rows_n, cols_n, count, ax, by)]
    all_to_all x1 -> x0, blocking collectives: 51 us -> none  [exchange(): lax.all_to_all(field, ('row', 'col'), split_axis=0, concat_axis=0, tiled=...]
    transpose x6 -> x0, local copies, waits for them, and re-layouts: 36.1 us -> none  [the longest x3 18.6 us: middle(): field = jnp.einsum('xi,kiy->kxy', basis_x, field, precision=FULL)]
    all_to_all x5 -> x0, starting transfers between devices: 23.8 us -> none  [exchange(): lax.all_to_all(field, ('row', 'col'), split_axis=0, concat_axis=0, tiled=...]
    dot_general x3 -> x0, local copies, waits for them, and re-layouts: 17 us -> none  [forward(): field = jnp.einsum('ck,abc->kab', columns(piece), source, precision=FAST)]
  transfers between devices with their start and end apart: 5 -> 0, of which waited for: 5 -> 0; matrix products, arithmetic and copies ran while one was open for 39% -> 0% of each run, Pallas kernels for 0% -> 0%
where the time goes in v1:
time: 739 us; the launch traced here: 737 us
  Pallas kernels  731 us (99%)
    pallas_call x1, Pallas kernels, fused_local(): pl.pallas_call(functools.partial(fused, rows_n, cols_n), out_shape=OUT_SH...  731 us

profile of v1, /device:TPU:9, one launch (start us, length us, event | category | flops | bytes accessed | tf_op | source)
XLA Modules:
  0.0 737.2 jit_solution(10383291953117248721)
XLA Ops:
  0.0 731.0 %shard_map.73 = f32[64,128,512]{2,1,0:T(8,128)S(1)} custom-call(f32[64,128,512]{2,1,0:T(8,128)} %source.1, f32[512,512]{1,0:T(8,128)} %basis_x.1, f32[512,512]{1,0:T(8,128)} %basis_y.1, f32[512,512]{1,0:T(8,128)} %basis_z.1, f32[1,512]{1,0:T(1,128)} %bitcast.2, f32[1,512]{1,0:T(1,128)} %bitcast.3, f32[512]{0:T(512)} %eigen_z.1), custom_call_target="tpu_custom_call" | custom-call | tf_op jit(solution)/shard_map/pallas_call | solution.py:217
  731.0 6.2 copy.9

commit v2 on v1

--- a/solution.py
+++ b/solution.py
@@ -13,8 +13,8 @@
 MESH = pl.DeviceIdType.MESH
 LANES = 128
 SUB = 8
-LIMIT = 46 << 20
-OUT_SHAPE = pltpu.VMEM
+LIMIT = 45 << 20
+TAIL_LIMIT = 20 << 20
 
 
 def split(value):
@@ -42,9 +42,9 @@
 def fused(
     rows_n, cols_n,
     source, basis_x, basis_y, basis_z, eigen_x, eigen_y, eigen_z,
-    out,
-    stage, arrived, z_high, z_low, x_high, x_low, xt_high, xt_low, y_high, y_low, yt_high, yt_low,
-    exy, load_sem, basis_sem, send1, recv1, send2, recv2, credit,
+    out, last, z_high, z_low,
+    stage, arrived, x_high, x_low, xt_high, xt_low, y_high, y_low, yt_high, yt_low,
+    exy, ex, ey, ez, eigen_sem, load_sem, basis_sem, send1, recv1, send2, recv2, credit,
 ):
     ax, by, nz = source.shape
     devices = rows_n * cols_n
@@ -73,22 +73,24 @@
     def basis_copy(ref, n):
         return pltpu.make_async_copy(ref.reshape(side, by, ref.shape[1]), out.at[basis_at(n)], basis_sem.at[n])
 
+    eigen = [(eigen_x, ex.at[0]), (eigen_y, ey.at[0]), (eigen_z, ez)]
+    eigen = [pltpu.make_async_copy(a, b, eigen_sem.at[n]) for n, (a, b) in enumerate(eigen)]
+
     basis_copy(basis_z, 0).start()
     load(0, 0).start()
-    load(1, 1).start()
-    basis_copy(basis_x, 1).start()
-    basis_copy(basis_y, 2).start()
-
     barrier = pltpu.get_barrier_semaphore()
     for r, c in order:
         if r or c:
             pl.semaphore_signal(barrier, inc=1, device_id=(row ^ r, col ^ c), device_id_type=MESH)
 
-    basis_copy(basis_z, 0).wait()
-    turned = out[basis_at(0)].reshape(nz, nz).T
-    for h in range(chunks):
+    def choose(h):
+        turned = out[basis_at(3)].reshape(nz, nz)
         rows = [turned[d * planes + h * SUB :][:SUB] for d in range(devices)]
         z_high[h], z_low[h] = split(jnp.concatenate(rows, axis=0))
+
+    basis_copy(basis_z, 0).wait()
+    out[basis_at(3)] = out[basis_at(0)].reshape(nz, nz).T.reshape(side, by, nz)
+    choose(0)
 
     def exchange(make_src, make_dst, send_sem, recv_sem):
         for r, c in order:
@@ -109,35 +111,48 @@
         view = ref.at[pl.ds(0, count)]
         pltpu.make_async_copy(view, view, sem).wait()
 
-    pl.semaphore_wait(barrier, devices - 1)
-
-    @pl.loop(0, chunks * groups)
-    def _(step):
+    def forward(step):
         h, g, slot = step // groups, lax.rem(step, groups), lax.rem(step, 2)
         load(step, slot).wait()
-
-        @pl.loop(0, SUB // 2)
-        def _(pair):
-            a = pair * 2
-            lhs = (z_high[h], z_low[h])
-            rhs = split(out[pl.ds(slot * SUB + a, 2)].reshape(2 * by, nz))
-            field = product(lhs, rhs, ((1,), (1,)))
-            for n in range(2):
-                for d in range(devices):
-                    start = h * chunk_rows + (d % cols_n) * nx + (d // cols_n) * ax + g * SUB + a + n
-                    stage_flat[pl.ds(start, SUB, stride=cols_n * nx), :] = field[
-                        d * SUB : (d + 1) * SUB, n * by : (n + 1) * by
-                    ]
-
-        @pl.when(step + 2 < chunks * groups)
-        def _():
-            load(step + 2, slot).start()
-
+        lhs = (z_high[h], z_low[h])
+        rhs = split(out[pl.ds(slot * SUB, SUB)].reshape(SUB * by, nz))
+        field = product(lhs, rhs, ((1,), (1,)))
+        for n in range(SUB):
+            for d in range(devices):
+                start = h * chunk_rows + (d % cols_n) * nx + (d // cols_n) * ax + g * SUB + n
+                stage_flat[pl.ds(start, SUB, stride=cols_n * nx), :] = field[
+                    d * SUB : (d + 1) * SUB, n * by : (n + 1) * by
+                ]
+
+    def send_forward(step):
+        h, g = step // groups, lax.rem(step, groups)
         exchange(
             lambda r, c: block(stage, h, r, c, g),
             lambda: block(arrived, h, row, col, g),
             send1.at[h], recv1.at[h],
         )
+
+    start = jnp.int32(0)
+    forward(start)
+    pl.semaphore_wait(barrier, devices - 1)
+    send_forward(start)
+    load(1, 1).start()
+    load(2, 0).start()
+    basis_copy(basis_x, 1).start()
+    basis_copy(basis_y, 2).start()
+    for copy in eigen:
+        copy.start()
+    for h in range(1, chunks):
+        choose(h)
+
+    @pl.loop(1, chunks * groups)
+    def _(step):
+        forward(step)
+        send_forward(step)
+
+        @pl.when(step + 2 < chunks * groups)
+        def _():
+            load(step + 2, lax.rem(step, 2)).start()
 
     basis_copy(basis_x, 1).wait()
     basis_copy(basis_y, 2).wait()
@@ -145,7 +160,9 @@
         value = out[basis_at(n)].reshape(nx, nx)
         natural[0][...], natural[1][...] = split(value)
         turned_refs[0][...], turned_refs[1][...] = split(value.T)
-    exy[...] = jnp.broadcast_to(eigen_x[...], exy.shape).T + eigen_y[...]
+    for copy in eigen:
+        copy.wait()
+    exy[...] = jnp.broadcast_to(ex[...], exy.shape).T + ey[...]
 
     def both(pair):
         return pair[0][...], pair[1][...]
@@ -159,7 +176,7 @@
             field = jnp.concatenate([arrived[p, c] for c in range(cols_n)], axis=1)
             field = product(both((xt_high, xt_low)), split(field))
             field = product(split(field), both((y_high, y_low)))
-            field = field / (exy[...] + eigen_z[me * planes + p])
+            field = field / (exy[...] + ez[me * planes + p])
             field = product(split(field), both((yt_high, yt_low)))
             field = product(both((x_high, x_low)), split(field))
             for c in range(cols_n):
@@ -180,25 +197,48 @@
 
     for h in range(chunks):
 
-        @pl.loop(0, groups)
+        @pl.loop(0, groups - (h == chunks - 1))
         def _(g):
             wait_rows(arrived_flat, part * SUB, recv2.at[h, g])
-
-            @pl.loop(0, SUB // 2)
-            def _(pair):
-                a = g * SUB + pair * 2
-                sides = [
-                    arrived_flat[pl.ds(h * chunk_rows + a + n, part, stride=ax), :].T for n in range(2)
-                ]
-                lhs = split(jnp.concatenate(sides, axis=0))
-                field = product(lhs, (z_high[h], z_low[h])).reshape(2, by, nz)
-                if h:
-                    out[pl.ds(a, 2)] += field
-                else:
-                    out[pl.ds(a, 2)] = field
-
+            a = g * SUB
+            sides = [
+                arrived_flat[pl.ds(h * chunk_rows + a + n, part, stride=ax), :].T for n in range(SUB)
+            ]
+            field = backward(sides, z_high[h], z_low[h])
+            if h:
+                field = field + out[pl.ds(a, SUB)]
+            out[pl.ds(a, SUB)] = field
+
+    h, g = chunks - 1, groups - 1
+    wait_rows(arrived_flat, part * SUB, recv2.at[h, g])
+    for d in range(devices):
+        last[d] = lines[h, d, :, g * SUB :, :]
     for h in range(chunks):
         wait_rows(stage_flat, (devices - 1) * SUB * ax, send2.at[h])
+
+
+def backward(sides, z_high, z_low):
+    field = product(split(jnp.concatenate(sides, axis=0)), (z_high, z_low))
+    return field.reshape(len(sides), -1, field.shape[1])
+
+
+def finish(most, last, z_high, z_low, out, tail, sems):
+    groups = out.shape[0] // SUB
+    copies = [
+        pltpu.make_async_copy(most.at[pl.ds(g * SUB, SUB)], out.at[pl.ds(g * SUB, SUB)], sems.at[g])
+        for g in range(groups - 1)
+    ]
+    copies.append(pltpu.make_async_copy(tail, out.at[pl.ds((groups - 1) * SUB, SUB)], sems.at[groups - 1]))
+    for copy in copies[:-1]:
+        copy.start()
+    part = last.shape[0] * SUB
+    rows = last.reshape(part * SUB, last.shape[3])
+    sides = [rows[pl.ds(n, part, stride=SUB), :].T for n in range(SUB)]
+    field = backward(sides, z_high[z_high.shape[0] - 1], z_low[z_low.shape[0] - 1])
+    tail[...] = field + most[pl.ds((groups - 1) * SUB, SUB)]
+    copies[-1].start()
+    for copy in copies:
+        copy.wait()
 
 
 def fused_local(source, basis_x, basis_y, basis_z, eigen_x, eigen_y, eigen_z):
@@ -209,27 +249,37 @@
     planes = nz // devices
     chunks, groups = planes // SUB, ax // SUB
     dma, any_space = pltpu.SemaphoreType.DMA, pl.BlockSpec(memory_space=pl.ANY)
-    vmem, smem = pl.BlockSpec(memory_space=pltpu.VMEM), pl.BlockSpec(memory_space=pltpu.SMEM)
+    vmem = pl.BlockSpec(memory_space=pltpu.VMEM)
     field = pltpu.VMEM((planes, cols_n, nx, by), jnp.float32)
     zb = pltpu.VMEM((chunks, devices * SUB, nz), jnp.bfloat16)
     xb = pltpu.VMEM((nx, nx), jnp.bfloat16)
     yb = pltpu.VMEM((ny, ny), jnp.bfloat16)
-    result = pl.pallas_call(
+    results = pl.pallas_call(
         functools.partial(fused, rows_n, cols_n),
-        out_shape=OUT_SHAPE((ax, by, nz), jnp.float32),
-        in_specs=[any_space] * 4 + [vmem, vmem, smem],
-        out_specs=vmem,
+        out_shape=(
+            pltpu.VMEM((ax, by, nz), jnp.float32), pltpu.VMEM((devices, SUB, SUB, by), jnp.float32), zb, zb,
+        ),
+        in_specs=[any_space] * 7,
+        out_specs=(vmem,) * 4,
         scratch_shapes=[
-            field, field, zb, zb, xb, xb, xb, xb, yb, yb, yb, yb,
-            pltpu.VMEM((nx, ny), jnp.float32),
-            dma((2,)), dma((3,)), dma((chunks,)), dma((chunks,)), dma((chunks,)), dma((chunks, groups)),
+            field, field, xb, xb, xb, xb, yb, yb, yb, yb,
+            pltpu.VMEM((nx, ny), jnp.float32), pltpu.VMEM((1, nx), jnp.float32), pltpu.VMEM((1, ny), jnp.float32),
+            pltpu.SMEM((nz,), jnp.float32),
+            dma((3,)), dma((2,)), dma((3,)), dma((chunks,)), dma((chunks,)), dma((chunks,)), dma((chunks, groups)),
             pltpu.SemaphoreType.REGULAR((chunks,)),
         ],
         compiler_params=pltpu.CompilerParams(
             collective_id=0, has_side_effects=True, vmem_limit_bytes=LIMIT
         ),
-    )(source, basis_x, basis_y, basis_z, eigen_x[None], eigen_y[None], eigen_z)
-    return result
+    )(source, basis_x, basis_y, basis_z, eigen_x, eigen_y, eigen_z)
+    return pl.pallas_call(
+        finish,
+        out_shape=jax.ShapeDtypeStruct((ax, by, nz), jnp.float32),
+        in_specs=[vmem] * 4,
+        out_specs=any_space,
+        scratch_shapes=[pltpu.VMEM((SUB, by, nz), jnp.float32), dma((groups,))],
+        compiler_params=pltpu.CompilerParams(vmem_limit_bytes=TAIL_LIMIT),
+    )(*results)
 
 
 def cuts(planes):
@@ -320,7 +370,7 @@
         square = basis_x.shape == basis_y.shape == basis_z.shape
         planes = nz // (rows_n * cols_n)
         power = not (rows_n & (rows_n - 1) or cols_n & (cols_n - 1))
-        fits = by == LANES and ax % SUB == 0 and planes % SUB == 0
+        fits = by == LANES and nz * ax >= 4 * SUB * SUB * rows_n * cols_n and ax % SUB == 0 and planes % SUB == 0
         body = fused_local if square and power and fits else staged_local
         return body(source, basis_x, basis_y, basis_z, *eigen)
 

time: 739 us -> 735 us (level)
    pallas_call x1 -> x2, Pallas kernels: 731 us -> 733 us  [the longest x1 727 us: fused_local(): pl.pallas_call(functools.partial(fused, rows_n, cols_n), out_shape=(pltpu...]
where the time goes in v2:
time: 735 us; the launch traced here: 733 us
  Pallas kernels  733 us (100%)
    pallas_call x1, Pallas kernels, fused_local(): pl.pallas_call(functools.partial(fused, rows_n, cols_n), out_shape=(pltpu...  727 us

profile of v2, /device:TPU:9, one launch (start us, length us, event | category | flops | bytes accessed | tf_op | source)
XLA Modules:
  0.0 732.9 jit_solution(8568047274659290645)
XLA Ops:
  0.0 727.0 %shard_map.73 = (f32[64,128,512]{2,1,0:T(8,128)S(1)}, f32[32,8,8,128]{3,2,1,0:T(8,128)S(1)}, bf16[2,256,512]{2,1,0:T(8,128)(2,1)S(1)}, bf16[2,256,512]{2,1,0:T(8,128)(2,1)S(1)}) custom-call(f32[64,128,512]{2,1,0:T(8,128)} %source.1, f32[512,512]{1,0:T(8,128)} %basis_x.1, f32[512,512]{1,0:T(8,128)} %basis_y.1, f32[512,512]{1,0:T(8,128)} %basis_z.1, ...), custom_call_target="tpu_custom_call" | custom-call | tf_op jit(solution)/shard_map/pallas_call | solution.py:257
  727.0 5.9 shard_map.74

commit v3 on v2

--- a/solution.py
+++ b/solution.py
@@ -59,16 +59,17 @@
     lines = arrived.reshape(chunks, devices, SUB, ax, by)
     chunk_rows = SUB * cols_n * nx
 
-    def load(step, slot):
-        g = lax.rem(step, groups)
-        return pltpu.make_async_copy(
-            source.at[pl.ds(g * SUB, SUB)], out.at[pl.ds(slot * SUB, SUB)], load_sem.at[slot]
-        )
-
-    side = nx // by
+    side, depth = nx // by, (ax - 4 * (nx // by)) // SUB
+
+    def slot_at(step):
+        return pl.ds(4 * side + lax.rem(step, depth) * SUB, SUB)
+
+    def load(step):
+        rows = pl.ds(lax.rem(step, groups) * SUB, SUB)
+        return pltpu.make_async_copy(source.at[rows], out.at[slot_at(step)], load_sem.at[lax.rem(step, depth)])
 
     def basis_at(n):
-        return pl.ds(2 * SUB + n * side, side)
+        return pl.ds(n * side, side)
 
     def basis_copy(ref, n):
         return pltpu.make_async_copy(ref.reshape(side, by, ref.shape[1]), out.at[basis_at(n)], basis_sem.at[n])
@@ -77,7 +78,7 @@
     eigen = [pltpu.make_async_copy(a, b, eigen_sem.at[n]) for n, (a, b) in enumerate(eigen)]
 
     basis_copy(basis_z, 0).start()
-    load(0, 0).start()
+    load(jnp.int32(0)).start()
     barrier = pltpu.get_barrier_semaphore()
     for r, c in order:
         if r or c:
@@ -90,10 +91,12 @@
 
     basis_copy(basis_z, 0).wait()
     out[basis_at(3)] = out[basis_at(0)].reshape(nz, nz).T.reshape(side, by, nz)
+    for n in range(1, depth):
+        load(jnp.int32(n)).start()
     choose(0)
 
-    def exchange(make_src, make_dst, send_sem, recv_sem):
-        for r, c in order:
+    def exchange(make_src, make_dst, send_sem, recv_sem, offsets=order):
+        for r, c in offsets:
             r2, c2 = row ^ r, col ^ c
             if r or c:
                 pltpu.make_async_remote_copy(
@@ -112,10 +115,10 @@
         pltpu.make_async_copy(view, view, sem).wait()
 
     def forward(step):
-        h, g, slot = step // groups, lax.rem(step, groups), lax.rem(step, 2)
-        load(step, slot).wait()
+        h, g = step // groups, lax.rem(step, groups)
+        load(step).wait()
         lhs = (z_high[h], z_low[h])
-        rhs = split(out[pl.ds(slot * SUB, SUB)].reshape(SUB * by, nz))
+        rhs = split(out[slot_at(step)].reshape(SUB * by, nz))
         field = product(lhs, rhs, ((1,), (1,)))
         for n in range(SUB):
             for d in range(devices):
@@ -123,6 +126,7 @@
                 stage_flat[pl.ds(start, SUB, stride=cols_n * nx), :] = field[
                     d * SUB : (d + 1) * SUB, n * by : (n + 1) * by
                 ]
+        pl.when(step + depth < chunks * groups)(lambda: load(step + depth).start())
 
     def send_forward(step):
         h, g = step // groups, lax.rem(step, groups)
@@ -136,8 +140,6 @@
     forward(start)
     pl.semaphore_wait(barrier, devices - 1)
     send_forward(start)
-    load(1, 1).start()
-    load(2, 0).start()
     basis_copy(basis_x, 1).start()
     basis_copy(basis_y, 2).start()
     for copy in eigen:
@@ -149,10 +151,6 @@
     def _(step):
         forward(step)
         send_forward(step)
-
-        @pl.when(step + 2 < chunks * groups)
-        def _():
-            load(step + 2, lax.rem(step, 2)).start()
 
     basis_copy(basis_x, 1).wait()
     basis_copy(basis_y, 2).wait()
@@ -187,13 +185,23 @@
                 pl.semaphore_signal(credit.at[h], inc=1, device_id=(row ^ r, col ^ c), device_id_type=MESH)
         pl.semaphore_wait(credit.at[h], devices - 1)
 
-        @pl.loop(0, groups)
-        def _(g):
+        def send_back(g, offsets=order):
             exchange(
                 lambda r, c: block(stage, h, r, c, g),
-                lambda: lines.at[h, me, :, pl.ds(g * SUB, SUB), :],
-                send2.at[h], recv2.at[h, g],
+                lambda: lines.at[h, me, :, pl.ds(pl.multiple_of(g * SUB, SUB), SUB), :],
+                send2.at[h], recv2.at[h, g], offsets,
             )
+
+        final = h == chunks - 1
+
+        @pl.loop(0, groups - final)
+        def _(g):
+            send_back(g)
+
+        if final:
+            half = cols_n // 2
+            columns = [*range(half, cols_n), *reversed(range(half))]
+            send_back(groups - 1, [(r, c) for c in columns for r in range(rows_n)])
 
     for h in range(chunks):
 
@@ -223,19 +231,20 @@
 
 
 def finish(most, last, z_high, z_low, out, tail, sems):
-    groups = out.shape[0] // SUB
+    start = out.shape[0] - SUB
+    step = start // (sems.shape[0] - 1)
     copies = [
-        pltpu.make_async_copy(most.at[pl.ds(g * SUB, SUB)], out.at[pl.ds(g * SUB, SUB)], sems.at[g])
-        for g in range(groups - 1)
+        pltpu.make_async_copy(most.at[pl.ds(n * step, step)], out.at[pl.ds(n * step, step)], sems.at[n])
+        for n in range(sems.shape[0] - 1)
     ]
-    copies.append(pltpu.make_async_copy(tail, out.at[pl.ds((groups - 1) * SUB, SUB)], sems.at[groups - 1]))
+    copies.append(pltpu.make_async_copy(tail, out.at[pl.ds(start, SUB)], sems.at[sems.shape[0] - 1]))
     for copy in copies[:-1]:
         copy.start()
     part = last.shape[0] * SUB
     rows = last.reshape(part * SUB, last.shape[3])
     sides = [rows[pl.ds(n, part, stride=SUB), :].T for n in range(SUB)]
     field = backward(sides, z_high[z_high.shape[0] - 1], z_low[z_low.shape[0] - 1])
-    tail[...] = field + most[pl.ds((groups - 1) * SUB, SUB)]
+    tail[...] = field + most[pl.ds(start, SUB)]
     copies[-1].start()
     for copy in copies:
         copy.wait()
@@ -265,7 +274,7 @@
             field, field, xb, xb, xb, xb, yb, yb, yb, yb,
             pltpu.VMEM((nx, ny), jnp.float32), pltpu.VMEM((1, nx), jnp.float32), pltpu.VMEM((1, ny), jnp.float32),
             pltpu.SMEM((nz,), jnp.float32),
-            dma((3,)), dma((2,)), dma((3,)), dma((chunks,)), dma((chunks,)), dma((chunks,)), dma((chunks, groups)),
+            dma((3,)), dma(((ax - 4 * (nx // by)) // SUB,)), dma((3,)), dma((chunks,)), dma((chunks,)), dma((chunks,)), dma((chunks, groups)),
             pltpu.SemaphoreType.REGULAR((chunks,)),
         ],
         compiler_params=pltpu.CompilerParams(
@@ -277,7 +286,7 @@
         out_shape=jax.ShapeDtypeStruct((ax, by, nz), jnp.float32),
         in_specs=[vmem] * 4,
         out_specs=any_space,
-        scratch_shapes=[pltpu.VMEM((SUB, by, nz), jnp.float32), dma((groups,))],
+        scratch_shapes=[pltpu.VMEM((SUB, by, nz), jnp.float32), dma((2 * groups - 1,))],
         compiler_params=pltpu.CompilerParams(vmem_limit_bytes=TAIL_LIMIT),
     )(*results)
 
@@ -370,7 +379,8 @@
         square = basis_x.shape == basis_y.shape == basis_z.shape
         planes = nz // (rows_n * cols_n)
         power = not (rows_n & (rows_n - 1) or cols_n & (cols_n - 1))
-        fits = by == LANES and nz * ax >= 4 * SUB * SUB * rows_n * cols_n and ax % SUB == 0 and planes % SUB == 0
+        room = 4 * (basis_x.shape[0] // LANES) + SUB <= ax
+        fits = by == LANES and room and ax % SUB == 0 and planes % SUB == 0
         body = fused_local if square and power and fits else staged_local
         return body(source, basis_x, basis_y, basis_z, *eigen)
 

time: 735 us -> 733 us (level)
  no operation moved by 1% of the time
where the time goes in v3:
time: 733 us
  Pallas kernels  733 us (100%)
    pallas_call x1, Pallas kernels, fused_local(): pl.pallas_call(functools.partial(fused, rows_n, cols_n), out_shape=(pltpu...  727 us

profile of v3, /device:TPU:9, one launch (start us, length us, event | category | flops | bytes accessed | tf_op | source)
XLA Modules:
  0.0 733.0 jit_solution(1871785095996234766)
XLA Ops:
  0.0 727.0 %shard_map.73 = (f32[64,128,512]{2,1,0:T(8,128)S(1)}, f32[32,8,8,128]{3,2,1,0:T(8,128)S(1)}, bf16[2,256,512]{2,1,0:T(8,128)(2,1)S(1)}, bf16[2,256,512]{2,1,0:T(8,128)(2,1)S(1)}) custom-call(f32[64,128,512]{2,1,0:T(8,128)} %source.1, f32[512,512]{1,0:T(8,128)} %basis_x.1, f32[512,512]{1,0:T(8,128)} %basis_y.1, f32[512,512]{1,0:T(8,128)} %basis_z.1, ...), custom_call_target="tpu_custom_call" | custom-call | tf_op jit(solution)/shard_map/pallas_call | solution.py:266
  727.0 6.0 shard_map.74

commit v4 on v3

--- a/solution.py
+++ b/solution.py
@@ -91,8 +91,6 @@
 
     basis_copy(basis_z, 0).wait()
     out[basis_at(3)] = out[basis_at(0)].reshape(nz, nz).T.reshape(side, by, nz)
-    for n in range(1, depth):
-        load(jnp.int32(n)).start()
     choose(0)
 
     def exchange(make_src, make_dst, send_sem, recv_sem, offsets=order):
@@ -114,9 +112,11 @@
         view = ref.at[pl.ds(0, count)]
         pltpu.make_async_copy(view, view, sem).wait()
 
-    def forward(step):
+    def forward(step, first=False):
         h, g = step // groups, lax.rem(step, groups)
         load(step).wait()
+        for n in range(1, depth if first else 1):
+            load(jnp.int32(n)).start()
         lhs = (z_high[h], z_low[h])
         rhs = split(out[slot_at(step)].reshape(SUB * by, nz))
         field = product(lhs, rhs, ((1,), (1,)))
@@ -137,7 +137,7 @@
         )
 
     start = jnp.int32(0)
-    forward(start)
+    forward(start, first=True)
     pl.semaphore_wait(barrier, devices - 1)
     send_forward(start)
     basis_copy(basis_x, 1).start()
@@ -185,10 +185,13 @@
                 pl.semaphore_signal(credit.at[h], inc=1, device_id=(row ^ r, col ^ c), device_id_type=MESH)
         pl.semaphore_wait(credit.at[h], devices - 1)
 
-        def send_back(g, offsets=order):
+        def line(g):
+            return lines.at[h, me, :, pl.ds(pl.multiple_of(g * SUB, SUB), SUB), :]
+
+        def send_back(g, offsets=order, target=line):
             exchange(
                 lambda r, c: block(stage, h, r, c, g),
-                lambda: lines.at[h, me, :, pl.ds(pl.multiple_of(g * SUB, SUB), SUB), :],
+                lambda: target(g),
                 send2.at[h], recv2.at[h, g], offsets,
             )
 
@@ -201,7 +204,7 @@
         if final:
             half = cols_n // 2
             columns = [*range(half, cols_n), *reversed(range(half))]
-            send_back(groups - 1, [(r, c) for c in columns for r in range(rows_n)])
+            send_back(groups - 1, [(r, c) for c in columns for r in range(rows_n)], lambda g: last.at[me])
 
     for h in range(chunks):
 
@@ -218,9 +221,7 @@
             out[pl.ds(a, SUB)] = field
 
     h, g = chunks - 1, groups - 1
-    wait_rows(arrived_flat, part * SUB, recv2.at[h, g])
-    for d in range(devices):
-        last[d] = lines[h, d, :, g * SUB :, :]
+    pltpu.make_async_copy(last, last, recv2.at[h, g]).wait()
     for h in range(chunks):
         wait_rows(stage_flat, (devices - 1) * SUB * ax, send2.at[h])
 

time: 733 us -> 733 us (level)
  no operation moved by 1% of the time
where the time goes in v4:
time: 733 us
  Pallas kernels  733 us (100%)
    pallas_call x1, Pallas kernels, fused_local(): pl.pallas_call(functools.partial(fused, rows_n, cols_n), out_shape=(pltpu...  727 us

profile of v4, /device:TPU:9, one launch (start us, length us, event | category | flops | bytes accessed | tf_op | source)
XLA Modules:
  0.0 732.9 jit_solution(9176179650904090005)
XLA Ops:
  0.0 726.9 %shard_map.73 = (f32[64,128,512]{2,1,0:T(8,128)S(1)}, f32[32,8,8,128]{3,2,1,0:T(8,128)S(1)}, bf16[2,256,512]{2,1,0:T(8,128)(2,1)S(1)}, bf16[2,256,512]{2,1,0:T(8,128)(2,1)S(1)}) custom-call(f32[64,128,512]{2,1,0:T(8,128)} %source.1, f32[512,512]{1,0:T(8,128)} %basis_x.1, f32[512,512]{1,0:T(8,128)} %basis_y.1, f32[512,512]{1,0:T(8,128)} %basis_z.1, ...), custom_call_target="tpu_custom_call" | custom-call | tf_op jit(solution)/shard_map/pallas_call | solution.py:267
  726.9 6.0 shard_map.74
